TPU v7x, 32 devices: a whole 2x2x4 slice. The times are simulated.
32 devices in a mesh: seq: 8 (over z, x), head: 4 (over y, core).
Axes of the slice: x: 2, y: 2, z: 4, core: 2. Of those that a mesh axis runs over, the one named last changes fastest.
Arguments:
- video_q: bfloat16 [1024, 4096], P(('seq', 'head')), may hold values from -200 to 200
- video_k: bfloat16 [1024, 4096], P(('seq', 'head')), may hold values from -6 to 6
- video_v: bfloat16 [1024, 4096], P(('seq', 'head')), may hold values from -6 to 6
- text_k: bfloat16 [512, 4096], P(None, 'head'), may hold values from -6 to 6
- text_v: bfloat16 [512, 4096], P(None, 'head'), may hold values from -6 to 6
- out_weight: bfloat16 [4096, 5120], P('head'), may hold values from -0.09375 to 0.09375
Outputs:
- video_out: bfloat16 [1024, 5120], P(('seq', 'head'))
All inputs are finite; a program needn't handle non-finite values.
Results may differ from a plain program's by a relative error of at most 0.018.
Values may be sent and summed in bfloat16 or wider, within the bound.
A program may use at most 128 MiB of HBM per device.

v0:
```python
import jax
import jax.numpy as jnp
from jax import lax
from jax.sharding import PartitionSpec as P

HD = 128


def as_heads(array):
    return array.reshape(array.shape[0], array.shape[1] // HD, HD)


def scores_of(query_heads, key_heads):
    return jnp.einsum(
        "qhd,khd->hqk", query_heads, key_heads, preferred_element_type=jnp.float32
    ) * HD ** (-0.5)


def weigh_values(scores, row_max, value_heads):
    weights = jnp.exp(scores - row_max[..., None]).astype(jnp.bfloat16)
    totals = jnp.sum(weights.astype(jnp.float32), axis=2)
    summed = jnp.einsum("hqk,khd->hqd", weights, value_heads, preferred_element_type=jnp.float32)
    return (totals, summed)


def local_partial(query_heads, key_heads, value_heads):
    scores = scores_of(query_heads, key_heads)
    row_max = jnp.max(scores, axis=2)
    totals, summed = weigh_values(scores, row_max, value_heads)
    return (row_max, totals, summed)


def combine_partial(first, second):
    joint = jnp.maximum(first[0], second[0])
    first_factor = jnp.exp(first[0] - joint)
    second_factor = jnp.exp(second[0] - joint)
    totals = first[1] * first_factor + second[1] * second_factor
    summed = first[2] * first_factor[..., None] + second[2] * second_factor[..., None]
    return (joint, totals, summed)


def body(video_q, video_k, video_v, text_k, text_v, out_weight):
    queries, key_rows, value_rows = (
        lax.all_to_all(video_q, "head", split_axis=1, concat_axis=0, tiled=True),
        lax.all_to_all(video_k, "head", split_axis=1, concat_axis=0, tiled=True),
        lax.all_to_all(video_v, "head", split_axis=1, concat_axis=0, tiled=True),
    )
    rows_here = queries.shape[0]
    query_heads = as_heads(queries)
    text_part = local_partial(query_heads, as_heads(text_k), as_heads(text_v))
    merged = combine_partial(
        text_part,
        local_partial(
            query_heads,
            as_heads(lax.all_gather(key_rows, "seq", axis=0, tiled=True)),
            as_heads(lax.all_gather(value_rows, "seq", axis=0, tiled=True)),
        ),
    )
    normalized = merged[2] / merged[1][..., None]
    attended = normalized.transpose(1, 0, 2).reshape(rows_here, -1).astype(jnp.bfloat16)
    return lax.psum_scatter(
        jnp.dot(attended, out_weight, preferred_element_type=jnp.float32).astype(jnp.bfloat16),
        "head",
        scatter_dimension=0,
        tiled=True,
    )


def solution(mesh):
    in_specs = (
        P(("seq", "head"), None),
        P(("seq", "head"), None),
        P(("seq", "head"), None),
        P(None, "head"),
        P(None, "head"),
        P("head", None),
    )
    out_specs = P(("seq", "head"), None)
    return jax.shard_map(body, mesh=mesh, in_specs=in_specs, out_specs=out_specs, check_vma=False)
```

profile of v0, /device:TPU:0, one launch (start us, length us, event | category | flops | bytes accessed | tf_op | source)
XLA Modules:
  0.0 162.2 jit_solution(479309963512354271)
XLA Ops:
  6.5 1.1 copy.63
  7.7 10.2 %all_to_all.54 = bf16[32,4,1024]{2,0,1:T(8,128)(2,1)} all-to-all(bf16[32,4,1024]{2,0,1:T(8,128)(2,1)S(1)} %bitcast.80), channel_id=1, replica_groups=mesh['seq'=8,'head'=4] {'head'}, dimensions={1} | all-to-all | bytes 524288 | tf_op jit(solution)/shard_map/all_to_all | solution.py:45
  17.9 0.0 all-gather.5.cloned.1.call-start
  17.9 1.0 copy.62
  18.9 9.1 %all_to_all.55 = bf16[32,4,1024]{2,0,1:T(8,128)(2,1)} all-to-all(bf16[32,4,1024]{2,0,1:T(8,128)(2,1)S(1)} %bitcast.81), channel_id=1, replica_groups=mesh['seq'=8,'head'=4] {'head'}, dimensions={1} | all-to-all | bytes 524288 | tf_op jit(solution)/shard_map/all_to_all | solution.py:46
  28.0 0.7 copy.64
  28.7 3.4 %all-to-all-start = ((bf16[32,4,1024]{2,0,1:T(8,128)(2,1)}), bf16[32,4,1024]{2,0,1:T(8,128)(2,1)S(1)}, u32[]{:S(2)}, u32[]{:S(2)}) async-start(bf16[32,4,1024]{2,0,1:T(8,128)(2,1)} %bitcast.71), calls=%async_computation | async-start | bytes 524288 | tf_op jit(solution)/shard_map/all_to_all | solution.py:44
  32.1 0.0 reduce-scatter.2.cloned.1.call-start
  32.2 1.3 copy.39
  33.5 4.6 %all-to-all-done = bf16[32,4,1024]{2,0,1:T(8,128)(2,1)S(1)} async-done(((bf16[32,4,1024]{2,0,1:T(8,128)(2,1)}), bf16[32,4,1024]{2,0,1:T(8,128)(2,1)S(1)}, u32[]{:S(2)}, u32[]{:S(2)}) %all-to-all-start) | async-done | bytes 262176 | tf_op jit(solution)/shard_map/all_to_all | solution.py:44
  38.2 0.5 multiply_reduce_fusion.1
  38.7 0.6 convert_reduce_fusion.1
  39.3 28.5 %all-gather.3.cloned.1.call-done = bf16[1024,1024]{1,0:T(8,128)(2,1)} async-done(((bf16[128,1024]{1,0:T(8,128)(2,1)}), bf16[1024,1024]{1,0:T(8,128)(2,1)}) %all-gather.3.cloned.1.call-update) | async-done | bytes 2097168 | tf_op jit(solution)/shard_map/all_gather | solution.py:55
  67.8 3.9 %copy.33 = bf16[1024,1024]{0,1:T(8,128)(2,1)} copy(bf16[1024,1024]{1,0:T(8,128)(2,1)} %all-gather.3.cloned.1.call-done) | data formatting | bytes 4194304 | tf_op jit(solution)/shard_map/all_gather | solution.py:55
  71.7 2.4 %multiply_reduce_fusion = (f32[8,128]{1,0:T(8,128)S(1)}, f32[8,128,1024]{2,1,0:T(8,128)S(1)}) fusion(bf16[1024,8,128]{0,2,1:T(8,128)(2,1)} %bitcast.72, bf16[128,8,128]{2,1,0:T(8,128)(2,1)S(1)} %bitcast.75), kind=kOutput, calls=%fused_computation.3 | convolution fusion | flops 270531584 | bytes 6557696 | tf_op jit(solution)/shard_map/qhd,khd->hqk/dot_general | solution.py:14
  74.1 0.9 convert_reduce_fusion
  75.0 1.0 copy-done.1
  76.0 0.1 copy-done.2
  76.1 1.4 fusion
  77.5 40.0 %all-gather.5.cloned.1.call-done = bf16[1024,1024]{1,0:T(8,128)(2,1)} async-done(((bf16[128,1024]{1,0:T(8,128)(2,1)}), bf16[1024,1024]{1,0:T(8,128)(2,1)}) %all-gather.5.cloned.1.call-update) | async-done | bytes 2097168 | tf_op jit(solution)/shard_map/all_gather | solution.py:56
  117.6 2.9 %copy.37 = bf16[1024,1024]{0,1:T(8,128)(2,1)S(1)} copy(bf16[1024,1024]{1,0:T(8,128)(2,1)} %all-gather.5.cloned.1.call-done) | data formatting | bytes 4194304 | tf_op jit(solution)/shard_map/all_gather | solution.py:56
  120.4 3.4 %fusion.4 = bf16[128,8,128]{0,2,1:T(8,128)(2,1)S(1)} fusion(f32[128,8,128]{0,2,1:T(8,128)} %fusion, bf16[1024,8,128]{0,2,1:T(8,128)(2,1)S(1)} %bitcast.76, f32[8,128,1024]{2,1,0:T(8,128)} %copy-done.1, f32[8,128]{1,0:T(8,128)S(1)} %get-tuple-element.8, f32[128,8]{0,1:T(8,128)S(1)} %get-tuple-element.5, f32[128,8]{0,1:T(8,128)S(1)} %get-tuple-element.6), kind=kOutput, calls=%fused_computation.13 | convolution fusion | flops 272105472 | bytes 7090176 | tf_op jit(solution)/shard_map/hqk,khd->hqd/dot_general | solution.py:22
  123.8 6.6 %convolution_convert_fusion = bf16[128,5120]{1,0:T(8,128)(2,1)} fusion(bf16[128,1024]{0,1:T(8,128)(2,1)S(1)} %bitcast.82, bf16[1024,5120]{1,0:T(8,128)(2,1)} %param.11), kind=kOutput, calls=%fused_computation | convolution fusion | flops 1342832640 | bytes 12058624 | tf_op jit(solution)/shard_map/dot_general | solution.py:62
  130.5 25.1 %reduce-scatter.2.cloned.1.call-done = bf16[32,5120]{1,0:T(8,128)(2,1)} async-done(((bf16[128,5120]{1,0:T(8,128)(2,1)}), bf16[32,5120]{1,0:T(8,128)(2,1)}) %reduce-scatter.2.cloned.1.call-update) | async-done | bytes 327696 | tf_op jit(solution)/shard_map/reduce_scatter | solution.py:61
  (14 shorter events, 0.1 us)
Async XLA Ops:
  6.5 31.6 %copy-start = (bf16[512,1024]{1,0:T(8,128)(2,1)S(1)}, bf16[512,1024]{1,0:T(8,128)(2,1)}, u32[]{:S(2)}) copy-start(bf16[512,1024]{1,0:T(8,128)(2,1)} %param.9) | copy-start | bytes 3145732
  6.5 21.5 %copy-start.4 = (bf16[32,4096]{1,0:T(8,128)(2,1)S(1)}, bf16[32,4096]{1,0:T(8,128)(2,1)}, u32[]{:S(2)}) copy-start(bf16[32,4096]{1,0:T(8,128)(2,1)} %param.6) | copy-start | bytes 786436
  6.5 25.7 %copy-start.3 = (bf16[512,1024]{1,0:T(8,128)(2,1)S(1)}, bf16[512,1024]{1,0:T(8,128)(2,1)}, u32[]{:S(2)}) copy-start(bf16[512,1024]{1,0:T(8,128)(2,1)} %param.10) | copy-start | bytes 3145732
  6.5 61.2 %all-gather.3.cloned.1.call-start = ((), (), s32[]{:S(2)}) async-start(), calls=%async_computation.4 | async-start | bytes 2359296 | tf_op jit(solution)/shard_map/all_gather | solution.py:55
  17.9 99.7 %all-gather.5.cloned.1.call-start = ((), (), s32[]{:S(2)}) async-start(), calls=%async_computation.5 | async-start | bytes 2359296 | tf_op jit(solution)/shard_map/all_gather | solution.py:56
  28.7 9.4 %all-to-all-start = ((bf16[32,4,1024]{2,0,1:T(8,128)(2,1)}), bf16[32,4,1024]{2,0,1:T(8,128)(2,1)S(1)}, u32[]{:S(2)}, u32[]{:S(2)}) async-start(bf16[32,4,1024]{2,0,1:T(8,128)(2,1)} %bitcast.71), calls=%async_computation | async-start | bytes 524288 | tf_op jit(solution)/shard_map/all_to_all | solution.py:44
  32.1 123.5 %reduce-scatter.2.cloned.1.call-start = ((), (), s32[]{:S(2)}) async-start(), calls=%async_computation.6 | async-start | bytes 1638400 | tf_op jit(solution)/shard_map/reduce_scatter | solution.py:61
  74.1 1.9 %copy-start.1 = (f32[8,128,1024]{2,1,0:T(8,128)}, f32[8,128,1024]{2,1,0:T(8,128)S(1)}, u32[]{:S(2)}) copy-start(f32[8,128,1024]{2,1,0:T(8,128)S(1)} %get-tuple-element.9) | copy-start | bytes 12582916
  74.1 2.0 %copy-start.2 = (bf16[512,1024]{0,1:T(8,128)(2,1)S(1)}, bf16[512,1024]{0,1:T(8,128)(2,1)}, u32[]{:S(2)}) copy-start(bf16[512,1024]{0,1:T(8,128)(2,1)} %copy.39) | copy-start | bytes 3145732
Sparse Core Ops, SparseCore 0:
  18.0 49.7 all-gather.2
  69.9 47.6 all-gather.4
  130.6 24.9 reduce-scatter.1
where the time goes:
time: 163 us; the launch traced here: 162 us
  waiting for transfers between devices  98.2 us (60%)
  blocking collectives  19.3 us (12%)
  matrix products  14.4 us (9%)
  between operations  13.2 us (8%)
  local copies, waits for them, and re-layouts  12 us (7%)
  starting transfers between devices  3.49 us (2%)
    all_gather x1, waiting for transfers between devices, body(): lax.all_gather(value_rows, 'seq', axis=0, tiled=True)  40 us
    all_gather x1, waiting for transfers between devices, body(): lax.all_gather(key_rows, 'seq', axis=0, tiled=True)  28.5 us
    reduce_scatter x1, waiting for transfers between devices, body(): lax.psum_scatter(jnp.dot(attended, out_weight, preferred_element_type=jnp...  25.1 us
    all_to_all x1, blocking collectives, body(): lax.all_to_all(video_k, 'head', split_axis=1, concat_axis=0, tiled=True)  10.2 us
    all_to_all x1, blocking collectives, body(): lax.all_to_all(video_v, 'head', split_axis=1, concat_axis=0, tiled=True)  9.08 us
    dot_general x1, matrix products, body(): jnp.dot(attended, out_weight, preferred_element_type=jnp.float32)  6.62 us
    dot_general x2, matrix products, weigh_values(): jnp.einsum('hqk,khd->hqd', weights, value_heads, preferred_element_type=j...  4.87 us
    all_to_all x1, waiting for transfers between devices, body(): lax.all_to_all(video_q, 'head', split_axis=1, concat_axis=0, tiled=True)  4.57 us
  transfers between devices with their start and end apart: 4, of which 4 were waited for; matrix products, arithmetic and copies ran while one was open for 8% of the time, Pallas kernels for 0%

commit v1 on v0

--- a/solution.py
+++ b/solution.py
@@ -1,9 +1,227 @@
+import functools
+import math
+
 import jax
 import jax.numpy as jnp
 from jax import lax
+from jax.experimental import pallas as pl
+from jax.experimental.pallas import tpu as pltpu
 from jax.sharding import PartitionSpec as P
 
 HD = 128
+BF16 = jnp.bfloat16
+F32 = jnp.float32
+CORES = 2
+SCALE = HD ** (-0.5) * math.log2(math.e)
+
+
+def kernel(
+    n_seq, n_head, q_ref, k_ref, v_ref, tk_ref, tv_ref, w_ref, o_ref,
+    stage, kq, vals, tk, tv, w, probs, att_send, att, part, pair_in, y_send, y_in,
+    load_sem, text_sem, w_sem, kq_send, kq_recv, v_send, v_recv,
+    att_ssem, att_rsem, pair_ssem, pair_rsem, y_ssem, y_rsem,
+):
+    s, g = lax.axis_index("seq"), lax.axis_index("head")
+    core, chip = lax.rem(g, CORES), lax.div(g, CORES)
+    chips = n_head // CORES
+    rows = q_ref.shape[0]
+    n_cols = w_sem.shape[0]
+    width = w_ref.shape[1] // n_cols
+    per_chunk = probs.shape[1] // (CORES * rows)
+    chunks = n_seq // per_chunk
+
+    def lanes(block):
+        return pl.ds(pl.multiple_of(block * HD, HD), HD)
+
+    def cols(n):
+        return pl.ds(n * width, width)
+
+    loads = [
+        pltpu.make_async_copy(ref, stage.at[i], load_sem.at[i])
+        for i, ref in enumerate((k_ref, q_ref, v_ref))
+    ]
+    texts = [
+        pltpu.make_async_copy(tk_ref.at[:, lanes(s)], tk, text_sem.at[0]),
+        pltpu.make_async_copy(tv_ref.at[:, lanes(s)], tv, text_sem.at[1]),
+    ]
+    weights = [
+        pltpu.make_async_copy(w_ref.at[:, cols(n)], w.at[:, cols(n)], w_sem.at[n])
+        for n in range(n_cols)
+    ]
+    for copy in loads + texts + weights:
+        copy.start()
+
+    others = [
+        (lax.rem(s + d // n_head, n_seq), lax.rem(g + d % n_head, n_head))
+        for d in range(1, n_seq * n_head)
+    ]
+    barrier = pltpu.get_barrier_semaphore()
+    for ts, tg in others:
+        pl.semaphore_signal(
+            barrier, inc=1, device_id={"seq": ts, "head": tg},
+            device_id_type=pl.DeviceIdType.MESH,
+        )
+    pl.semaphore_wait(barrier, len(others))
+
+    def send(src, dst, ssem, rsem, ts, tg):
+        copy = pltpu.make_async_remote_copy(
+            src_ref=src, dst_ref=dst, send_sem=ssem, recv_sem=rsem,
+            device_id={"seq": ts, "head": tg}, device_id_type=pl.DeviceIdType.MESH,
+        )
+        copy.start()
+        return copy
+
+    def wait_for(ref, sem):
+        pltpu.make_async_copy(ref, ref, sem).wait()
+
+    loads[0].wait()
+    loads[1].wait()
+    for ts, tg in others:
+        send(stage.at[0:2, :, lanes(tg * n_seq + ts)], kq.at[:, s, g], kq_send, kq_recv, ts, tg)
+    mine = lanes(g * n_seq + s)
+    pltpu.make_async_copy(stage.at[0:2, :, mine], kq.at[:, s, g], kq_recv).start()
+    loads[2].wait()
+    for ts, tg in others:
+        send(stage.at[2, :, lanes(tg * n_seq + ts)], vals.at[s, g], v_send, v_recv, ts, tg)
+    pltpu.make_async_copy(stage.at[2, :, mine], vals.at[s, g], v_recv).start()
+
+    texts[0].wait()
+    wait_for(kq, kq_recv)
+    keyed = (((1,), (1,)), ((), ()))
+    passes = [(t, lax.rem(chip + t, chips)) for t in list(range(1, chips)) + [0]]
+    group = lax.div(s, per_chunk)
+    for order, (t, owner) in enumerate(passes):
+        blocks = [lax.rem(group + c + 1, chunks) * per_chunk for c in range(chunks)]
+        for c, first in enumerate(blocks):
+            q = kq[1, pl.ds(first, per_chunk), pl.ds(owner * CORES, CORES)]
+            q = q.reshape(per_chunk * CORES * rows, HD)
+            keys = kq[0].reshape(n_seq * n_head * rows, HD)
+            on_video = lax.dot_general(q, keys, keyed, preferred_element_type=F32)
+            on_text = lax.dot_general(q, tk[...], keyed, preferred_element_type=F32)
+            top = jnp.maximum(
+                jnp.max(on_video, axis=1, keepdims=True),
+                jnp.max(on_text, axis=1, keepdims=True),
+            )
+            split = keys.shape[0]
+            probs[c, :, :split] = jnp.exp2((on_video - top) * SCALE).astype(BF16)
+            probs[c, :, split:] = jnp.exp2((on_text - top) * SCALE).astype(BF16)
+        if order == 0:
+            texts[1].wait()
+            wait_for(vals, v_recv)
+        for c, first in enumerate(blocks):
+            values = vals[...].reshape(split, HD)
+            ahead = jnp.dot(
+                probs[c, :, :split],
+                jnp.concatenate([values, jnp.ones_like(values)], axis=1),
+                preferred_element_type=F32,
+            ) + jnp.dot(
+                probs[c, :, split:],
+                jnp.concatenate([tv[...], jnp.ones_like(tv)], axis=1),
+                preferred_element_type=F32,
+            )
+            done = (ahead[:, :HD] / ahead[:, HD:]).astype(BF16)
+            att_send[t, c] = done.reshape(per_chunk, CORES * rows, HD)
+            for b in range(per_chunk):
+                here = lax.rem(s + b, per_chunk) if c == chunks - 1 else b
+                src, dst = att_send.at[t, c, here], att.at[t, :, lanes(s)]
+                if c == chunks - 1 and b == 0:
+                    pltpu.make_async_copy(src, dst, att_rsem.at[t]).start()
+                else:
+                    send(src, dst, att_ssem.at[t], att_rsem.at[t], first + here, g)
+
+    other = g + 1 - 2 * core
+    crossing = []
+
+    def project(t, n):
+        if t == passes[0][0]:
+            weights[n].wait()
+        out = jnp.dot(att[t], w[:, cols(n)], preferred_element_type=F32).astype(BF16)
+        part[t, :, :, cols(n)] = out.reshape(CORES, rows, width)
+        return send(
+            part.at[t, 1 - core, :, cols(n)], pair_in.at[t, :, cols(n)],
+            pair_ssem.at[t, n], pair_rsem.at[t, n], s, other,
+        )
+
+    def own_sum(t, n, copy):
+        copy.wait()
+        return part[t, core, :, cols(n)].astype(F32) + pair_in[t, :, cols(n)].astype(F32)
+
+    def cross(t, owner, n, copy):
+        y_send[t - 1, :, cols(n)] = own_sum(t, n, copy).astype(BF16)
+        crossing.append((t, n, send(
+            y_send.at[t - 1, :, cols(n)], y_in.at[t - 1, :, cols(n)],
+            y_ssem.at[t - 1, n], y_rsem.at[t - 1, n], s, owner * CORES + core,
+        )))
+
+    LAG = 2
+    pending, last = [], []
+    for t, owner in passes:
+        wait_for(att.at[t], att_rsem.at[t])
+        for n in range(n_cols):
+            copy = project(t, n)
+            if t == 0:
+                last.append(copy)
+            else:
+                pending.append((t, owner, n, copy))
+            if len(pending) > LAG or (t == 0 and pending):
+                cross(*pending.pop(0))
+    while pending:
+        cross(*pending.pop(0))
+    for n in range(n_cols):
+        total = own_sum(0, n, last[n])
+        for t, m, copy in crossing:
+            if m == n:
+                copy.wait()
+                total = total + y_in[t - 1, :, cols(n)].astype(F32)
+        o_ref[:, cols(n)] = total.astype(BF16)
+
+    for i in range(2):
+        wait_for(kq.at[i].reshape(n_seq * n_head, rows, HD).at[1:], kq_send)
+    wait_for(vals.reshape(n_seq * n_head, rows, HD).at[1:], v_send)
+    for t, owner in passes:
+        wait_for(att.at[t, :, : (n_seq - 1) * HD], att_ssem.at[t])
+
+
+def fused(n_seq, n_head, video_q, video_k, video_v, text_k, text_v, out_weight):
+    rows, text = video_q.shape[0], text_k.shape[0]
+    depth, d = out_weight.shape
+    tokens = n_seq * n_head * rows
+    chips = n_head // CORES
+    per_chunk = 2
+    chunks = n_seq // per_chunk
+    m = per_chunk * CORES * rows
+    n_cols = next(n for n in (5, 4, 8, 2, 1) if d % (n * 2 * HD) == 0)
+    anywhere = pl.BlockSpec(memory_space=pl.ANY)
+    dma = pltpu.SemaphoreType.DMA
+    return pl.pallas_call(
+        functools.partial(kernel, n_seq, n_head),
+        out_shape=jax.ShapeDtypeStruct((rows, d), BF16),
+        in_specs=[anywhere] * 6,
+        out_specs=pl.BlockSpec(memory_space=pltpu.VMEM),
+        scratch_shapes=[
+            pltpu.VMEM((3, rows, video_q.shape[1]), BF16),
+            pltpu.VMEM((2, n_seq, n_head, rows, HD), BF16),
+            pltpu.VMEM((n_seq, n_head, rows, HD), BF16),
+            pltpu.VMEM((text, HD), BF16),
+            pltpu.VMEM((text, HD), BF16),
+            pltpu.VMEM((depth, d), BF16),
+            pltpu.VMEM((chunks, m, tokens + text), BF16),
+            pltpu.VMEM((chips, chunks, per_chunk, CORES * rows, HD), BF16),
+            pltpu.VMEM((chips, CORES * rows, depth), BF16),
+            pltpu.VMEM((chips, CORES, rows, d), BF16),
+            pltpu.VMEM((chips, rows, d), BF16),
+            pltpu.VMEM((max(chips - 1, 1), rows, d), BF16),
+            pltpu.VMEM((max(chips - 1, 1), rows, d), BF16),
+            dma((3,)), dma((2,)), dma((n_cols,)),
+            dma(()), dma(()), dma(()), dma(()),
+            dma((chips,)), dma((chips,)),
+            dma((chips, n_cols)), dma((chips, n_cols)),
+            dma((chips, n_cols)), dma((chips, n_cols)),
+        ],
+        compiler_params=pltpu.CompilerParams(
+            collective_id=0, has_side_effects=True, vmem_limit_bytes=60 * 2**20
+        ),
+    )(video_q, video_k, video_v, text_k, text_v, out_weight)
 
 
 def as_heads(array):
@@ -67,6 +285,13 @@
 
 
 def solution(mesh):
+    n_seq, n_head = mesh.shape["seq"], mesh.shape["head"]
+
+    def step(*arrays):
+        heads_here = arrays[3].shape[1] // HD
+        one_head_each = heads_here == n_seq and n_seq % 2 == 0 and n_head % CORES == 0
+        return fused(n_seq, n_head, *arrays) if one_head_each else body(*arrays)
+
     in_specs = (
         P(("seq", "head"), None),
         P(("seq", "head"), None),
@@ -76,4 +301,4 @@
         P("head", None),
     )
     out_specs = P(("seq", "head"), None)
-    return jax.shard_map(body, mesh=mesh, in_specs=in_specs, out_specs=out_specs, check_vma=False)
+    return jax.shard_map(step, mesh=mesh, in_specs=in_specs, out_specs=out_specs, check_vma=False)

time: 163 us -> 45.1 us (0.28)
  waiting for transfers between devices: 98.2 us -> 0 us
  Pallas kernels: 0 us -> 43.2 us
  blocking collectives: 19.3 us -> 0 us
  matrix products: 14.4 us -> 0 us
  between operations: 13.2 us -> 0.01 us
  local copies, waits for them, and re-layouts: 12 us -> 1.72 us
  starting transfers between devices: 3.49 us -> 0 us
    all_gather x2 -> x0, waiting for transfers between devices: 68.5 us -> none  [the longest x1 40 us: body(): lax.all_gather(value_rows, 'seq', axis=0, tiled=True)]
    pallas_call x0 -> x1, Pallas kernels: none -> 43.2 us  [fused(): pl.pallas_call(functools.partial(kernel, n_seq, n_head), out_shape=jax.Sh...]
    reduce_scatter x1 -> x0, waiting for transfers between devices: 25.1 us -> none  [body(): lax.psum_scatter(jnp.dot(attended, out_weight, preferred_element_type=jnp...]
    all_to_all x2 -> x0, blocking collectives: 19.3 us -> none  [the longest x1 10.2 us: body(): lax.all_to_all(video_k, 'head', split_axis=1, concat_axis=0, tiled=True)]
    dot_general x5 -> x0, matrix products: 14.4 us -> none  [the longest x1 6.62 us: body(): jnp.dot(attended, out_weight, preferred_element_type=jnp.float32)]
    all_gather x2 -> x0, local copies, waits for them, and re-layouts: 6.78 us -> none  [the longest x1 3.93 us: body(): lax.all_gather(key_rows, 'seq', axis=0, tiled=True)]
    all_to_all x1 -> x0, waiting for transfers between devices: 4.57 us -> none  [body(): lax.all_to_all(video_q, 'head', split_axis=1, concat_axis=0, tiled=True)]
    all_to_all x1 -> x0, starting transfers between devices: 3.41 us -> none  [body(): lax.all_to_all(video_q, 'head', split_axis=1, concat_axis=0, tiled=True)]
  transfers between devices with their start and end apart: 4 -> 0, of which waited for: 4 -> 0; matrix products, arithmetic and copies ran while one was open for 8% -> 0% of each run, Pallas kernels for 0% -> 0%
where the time goes in v1:
time: 45.1 us; the launch traced here: 44.9 us
  Pallas kernels  43.2 us (96%)
  local copies, waits for them, and re-layouts  1.72 us (4%)
    pallas_call x1, Pallas kernels, fused(): pl.pallas_call(functools.partial(kernel, n_seq, n_head), out_shape=jax.Sh...  43.2 us
    unnamed x1, local copies, waits for them, and re-layouts  1.72 us

profile of v1, /device:TPU:0, one launch (start us, length us, event | category | flops | bytes accessed | tf_op | source)
XLA Modules:
  0.0 44.9 jit_solution(17611894857616974108)
XLA Ops:
  0.0 43.2 %shard_map.64 = bf16[32,5120]{1,0:T(8,128)(2,1)} custom-call(bf16[32,4096]{1,0:T(8,128)(2,1)} %q_ref.1, bf16[32,4096]{1,0:T(8,128)(2,1)} %k_ref.1, bf16[32,4096]{1,0:T(8,128)(2,1)} %v_ref.1, bf16[512,1024]{1,0:T(8,128)(2,1)} %tk_ref.1, bf16[512,1024]{1,0:T(8,128)(2,1)} %tv_ref.1, bf16[1024,5120]{1,0:T(8,128)(2,1)} %w_ref.1), custom_call_target="tpu_custom_call" | custom-call | tf_op jit(solution)/shard_map/pallas_call | solution.py:196
  43.2 1.7 %copy.8 = bf16[32,5120]{1,0:T(8,128)(2,1)} copy(bf16[32,5120]{1,0:T(8,128)(2,1)} %shard_map.64) | data formatting | bytes 655360

commit v2 on v1

--- a/solution.py
+++ b/solution.py
@@ -17,8 +17,8 @@
 
 def kernel(
     n_seq, n_head, q_ref, k_ref, v_ref, tk_ref, tv_ref, w_ref, o_ref,
-    stage, kq, vals, tk, tv, w, probs, att_send, att, part, pair_in, y_send, y_in,
-    load_sem, text_sem, w_sem, kq_send, kq_recv, v_send, v_recv,
+    stage, keys_in, vals, queries, tk, tv, w, probs, att_send, att, part, pair_in, y_send, y_in,
+    load_sem, text_sem, w_sem, k_send, k_recv, v_send, v_recv, q_send, q_recv,
     att_ssem, att_rsem, pair_ssem, pair_rsem, y_ssem, y_rsem,
 ):
     s, g = lax.axis_index("seq"), lax.axis_index("head")
@@ -27,8 +27,9 @@
     rows = q_ref.shape[0]
     n_cols = w_sem.shape[0]
     width = w_ref.shape[1] // n_cols
-    per_chunk = probs.shape[1] // (CORES * rows)
+    per_chunk = probs.shape[1] // rows
     chunks = n_seq // per_chunk
+    split = n_seq * n_head * rows
 
     def lanes(block):
         return pl.ds(pl.multiple_of(block * HD, HD), HD)
@@ -51,9 +52,18 @@
     for copy in loads + texts + weights:
         copy.start()
 
+    turns = list(range(1, chips)) + [0]
+    offsets = list(range(n_seq))
+
+    def targets(turn):
+        return [
+            (lax.rem(s + o, n_seq), lax.rem(chip + chips - turn, chips) * CORES + lax.rem(core + c, CORES))
+            for o in offsets for c in range(CORES) if (turn, o, c) != (0, 0, 0)
+        ]
+
     others = [
-        (lax.rem(s + d // n_head, n_seq), lax.rem(g + d % n_head, n_head))
-        for d in range(1, n_seq * n_head)
+        (lax.rem(s + o, n_seq), lax.rem(chip + chips - turn, chips) * CORES + lax.rem(core + c, CORES))
+        for o in offsets for turn in turns for c in range(CORES) if (turn, o, c) != (0, 0, 0)
     ]
     barrier = pltpu.get_barrier_semaphore()
     for ts, tg in others:
@@ -64,45 +74,51 @@
     pl.semaphore_wait(barrier, len(others))
 
     def send(src, dst, ssem, rsem, ts, tg):
-        copy = pltpu.make_async_remote_copy(
+        return pltpu.make_async_remote_copy(
             src_ref=src, dst_ref=dst, send_sem=ssem, recv_sem=rsem,
             device_id={"seq": ts, "head": tg}, device_id_type=pl.DeviceIdType.MESH,
         )
-        copy.start()
-        return copy
 
     def wait_for(ref, sem):
         pltpu.make_async_copy(ref, ref, sem).wait()
 
+    mine = lanes(g * n_seq + s)
+
+    def spread(i, buffer, ssem, rsem, to):
+        for ts, tg in to:
+            send(stage.at[i, :, lanes(tg * n_seq + ts)], buffer.at[s, g], ssem, rsem, ts, tg).start()
+
     loads[0].wait()
+    spread(0, keys_in, k_send, k_recv, others)
+    pltpu.make_async_copy(stage.at[0, :, mine], keys_in.at[s, g], k_recv).start()
     loads[1].wait()
-    for ts, tg in others:
-        send(stage.at[0:2, :, lanes(tg * n_seq + ts)], kq.at[:, s, g], kq_send, kq_recv, ts, tg)
-    mine = lanes(g * n_seq + s)
-    pltpu.make_async_copy(stage.at[0:2, :, mine], kq.at[:, s, g], kq_recv).start()
+    for turn in turns[:-1]:
+        spread(1, queries, q_send.at[turn], q_recv.at[turn], targets(turn))
     loads[2].wait()
-    for ts, tg in others:
-        send(stage.at[2, :, lanes(tg * n_seq + ts)], vals.at[s, g], v_send, v_recv, ts, tg)
+    spread(2, vals, v_send, v_recv, others)
     pltpu.make_async_copy(stage.at[2, :, mine], vals.at[s, g], v_recv).start()
+    spread(1, queries, q_send.at[0], q_recv.at[0], targets(0))
+    pltpu.make_async_copy(stage.at[1, :, mine], queries.at[s, g], q_recv.at[0]).start()
 
     texts[0].wait()
-    wait_for(kq, kq_recv)
+    wait_for(keys_in, k_recv)
     keyed = (((1,), (1,)), ((), ()))
-    passes = [(t, lax.rem(chip + t, chips)) for t in list(range(1, chips)) + [0]]
     group = lax.div(s, per_chunk)
-    for order, (t, owner) in enumerate(passes):
-        blocks = [lax.rem(group + c + 1, chunks) * per_chunk for c in range(chunks)]
+    blocks = [lax.rem(group + c + 1, chunks) * per_chunk for c in range(chunks)]
+    owners = [(t, lax.rem(chip + t, chips)) for t in turns]
+    passes = [(t, owner, cc) for t, owner in owners for cc in range(CORES)]
+    for order, (t, owner, cc) in enumerate(passes):
+        if cc == 0:
+            wait_for(queries.at[:, pl.ds(owner * CORES, CORES)], q_recv.at[t])
         for c, first in enumerate(blocks):
-            q = kq[1, pl.ds(first, per_chunk), pl.ds(owner * CORES, CORES)]
-            q = q.reshape(per_chunk * CORES * rows, HD)
-            keys = kq[0].reshape(n_seq * n_head * rows, HD)
+            q = queries[pl.ds(first, per_chunk), owner * CORES + cc].reshape(per_chunk * rows, HD)
+            keys = keys_in[...].reshape(split, HD)
             on_video = lax.dot_general(q, keys, keyed, preferred_element_type=F32)
             on_text = lax.dot_general(q, tk[...], keyed, preferred_element_type=F32)
             top = jnp.maximum(
                 jnp.max(on_video, axis=1, keepdims=True),
                 jnp.max(on_text, axis=1, keepdims=True),
             )
-            split = keys.shape[0]
             probs[c, :, :split] = jnp.exp2((on_video - top) * SCALE).astype(BF16)
             probs[c, :, split:] = jnp.exp2((on_text - top) * SCALE).astype(BF16)
         if order == 0:
@@ -120,66 +136,76 @@
                 preferred_element_type=F32,
             )
             done = (ahead[:, :HD] / ahead[:, HD:]).astype(BF16)
-            att_send[t, c] = done.reshape(per_chunk, CORES * rows, HD)
+            att_send[t, cc, c] = done.reshape(per_chunk, rows, HD)
             for b in range(per_chunk):
                 here = lax.rem(s + b, per_chunk) if c == chunks - 1 else b
-                src, dst = att_send.at[t, c, here], att.at[t, :, lanes(s)]
+                src, dst = att_send.at[t, cc, c, here], att.at[t, cc, :, lanes(s)]
                 if c == chunks - 1 and b == 0:
-                    pltpu.make_async_copy(src, dst, att_rsem.at[t]).start()
+                    pltpu.make_async_copy(src, dst, att_rsem.at[t, cc]).start()
                 else:
-                    send(src, dst, att_ssem.at[t], att_rsem.at[t], first + here, g)
-
-    other = g + 1 - 2 * core
-    crossing = []
-
-    def project(t, n):
-        if t == passes[0][0]:
-            weights[n].wait()
-        out = jnp.dot(att[t], w[:, cols(n)], preferred_element_type=F32).astype(BF16)
-        part[t, :, :, cols(n)] = out.reshape(CORES, rows, width)
+                    send(src, dst, att_ssem.at[t, cc], att_rsem.at[t, cc], first + here, g).start()
+
+    def to_pair(t, n):
         return send(
             part.at[t, 1 - core, :, cols(n)], pair_in.at[t, :, cols(n)],
-            pair_ssem.at[t, n], pair_rsem.at[t, n], s, other,
+            pair_ssem.at[t, n], pair_rsem.at[t, n], s, g + 1 - 2 * core,
         )
 
-    def own_sum(t, n, copy):
-        copy.wait()
-        return part[t, core, :, cols(n)].astype(F32) + pair_in[t, :, cols(n)].astype(F32)
-
-    def cross(t, owner, n, copy):
-        y_send[t - 1, :, cols(n)] = own_sum(t, n, copy).astype(BF16)
-        crossing.append((t, n, send(
+    def to_owner(t, owner, n):
+        return send(
             y_send.at[t - 1, :, cols(n)], y_in.at[t - 1, :, cols(n)],
             y_ssem.at[t - 1, n], y_rsem.at[t - 1, n], s, owner * CORES + core,
-        )))
+        )
+
+    def own_sum(t, n):
+        to_pair(t, n).wait_recv()
+        return part[t, core, :, cols(n)].astype(F32) + pair_in[t, :, cols(n)].astype(F32)
+
+    def cross(t, owner, cc, n):
+        @pl.when(core == cc)
+        def _():
+            y_send[t - 1, :, cols(n)] = own_sum(t, n).astype(BF16)
+            to_owner(t, owner, n).start()
 
     LAG = 2
-    pending, last = [], []
-    for t, owner in passes:
-        wait_for(att.at[t], att_rsem.at[t])
+    pending = []
+    for order, (t, owner, cc) in enumerate(passes):
+        wait_for(att.at[t, cc], att_rsem.at[t, cc])
         for n in range(n_cols):
-            copy = project(t, n)
-            if t == 0:
-                last.append(copy)
-            else:
-                pending.append((t, owner, n, copy))
-            if len(pending) > LAG or (t == 0 and pending):
+            if order == 0:
+                weights[n].wait()
+            part[t, cc, :, cols(n)] = jnp.dot(
+                att[t, cc], w[:, cols(n)], preferred_element_type=F32
+            ).astype(BF16)
+
+            @pl.when(core != cc)
+            def _():
+                to_pair(t, n).start()
+
+            if t > 0:
+                pending.append((t, owner, cc, n))
+            if pending and (len(pending) > LAG or t == 0):
                 cross(*pending.pop(0))
     while pending:
         cross(*pending.pop(0))
     for n in range(n_cols):
-        total = own_sum(0, n, last[n])
-        for t, m, copy in crossing:
-            if m == n:
-                copy.wait()
-                total = total + y_in[t - 1, :, cols(n)].astype(F32)
+        total = own_sum(0, n)
+        for t, owner in owners[:-1]:
+            to_owner(t, owner, n).wait_recv()
+            total = total + y_in[t - 1, :, cols(n)].astype(F32)
         o_ref[:, cols(n)] = total.astype(BF16)
 
-    for i in range(2):
-        wait_for(kq.at[i].reshape(n_seq * n_head, rows, HD).at[1:], kq_send)
-    wait_for(vals.reshape(n_seq * n_head, rows, HD).at[1:], v_send)
-    for t, owner in passes:
-        wait_for(att.at[t, :, : (n_seq - 1) * HD], att_ssem.at[t])
+    for buffer, sem in ((keys_in, k_send), (vals, v_send)):
+        wait_for(buffer.reshape(n_seq * n_head, rows, HD).at[1:], sem)
+    for t, owner in owners:
+        sent = n_seq * CORES - (t == 0)
+        wait_for(queries.reshape(n_seq * n_head, rows, HD).at[:sent], q_send.at[t])
+        for cc in range(CORES):
+            wait_for(att.at[t, cc, :, : (n_seq - 1) * HD], att_ssem.at[t, cc])
+        for n in range(n_cols):
+            to_pair(t, n).wait_send()
+            if t > 0:
+                to_owner(t, owner, n).wait_send()
 
 
 def fused(n_seq, n_head, video_q, video_k, video_v, text_k, text_v, out_weight):
@@ -187,10 +213,10 @@
     depth, d = out_weight.shape
     tokens = n_seq * n_head * rows
     chips = n_head // CORES
-    per_chunk = 2
+    per_chunk = next(c for c in (4, 2, 1) if n_seq % c == 0)
     chunks = n_seq // per_chunk
-    m = per_chunk * CORES * rows
-    n_cols = next(n for n in (5, 4, 8, 2, 1) if d % (n * 2 * HD) == 0)
+    m = per_chunk * rows
+    n_cols = next(n for n in (4, 5, 8, 2, 1) if d % (n * 2 * HD) == 0)
     anywhere = pl.BlockSpec(memory_space=pl.ANY)
     dma = pltpu.SemaphoreType.DMA
     return pl.pallas_call(
@@ -200,21 +226,22 @@
         out_specs=pl.BlockSpec(memory_space=pltpu.VMEM),
         scratch_shapes=[
             pltpu.VMEM((3, rows, video_q.shape[1]), BF16),
-            pltpu.VMEM((2, n_seq, n_head, rows, HD), BF16),
+            pltpu.VMEM((n_seq, n_head, rows, HD), BF16),
+            pltpu.VMEM((n_seq, n_head, rows, HD), BF16),
             pltpu.VMEM((n_seq, n_head, rows, HD), BF16),
             pltpu.VMEM((text, HD), BF16),
             pltpu.VMEM((text, HD), BF16),
             pltpu.VMEM((depth, d), BF16),
             pltpu.VMEM((chunks, m, tokens + text), BF16),
-            pltpu.VMEM((chips, chunks, per_chunk, CORES * rows, HD), BF16),
-            pltpu.VMEM((chips, CORES * rows, depth), BF16),
+            pltpu.VMEM((chips, CORES, chunks, per_chunk, rows, HD), BF16),
+            pltpu.VMEM((chips, CORES, rows, depth), BF16),
             pltpu.VMEM((chips, CORES, rows, d), BF16),
             pltpu.VMEM((chips, rows, d), BF16),
             pltpu.VMEM((max(chips - 1, 1), rows, d), BF16),
             pltpu.VMEM((max(chips - 1, 1), rows, d), BF16),
             dma((3,)), dma((2,)), dma((n_cols,)),
-            dma(()), dma(()), dma(()), dma(()),
-            dma((chips,)), dma((chips,)),
+            dma(()), dma(()), dma(()), dma(()), dma((chips,)), dma((chips,)),
+            dma((chips, CORES)), dma((chips, CORES)),
             dma((chips, n_cols)), dma((chips, n_cols)),
             dma((chips, n_cols)), dma((chips, n_cols)),
         ],
@@ -289,7 +316,7 @@
 
     def step(*arrays):
         heads_here = arrays[3].shape[1] // HD
-        one_head_each = heads_here == n_seq and n_seq % 2 == 0 and n_head % CORES == 0
+        one_head_each = heads_here == n_seq and n_head % CORES == 0
         return fused(n_seq, n_head, *arrays) if one_head_each else body(*arrays)
 
     in_specs = (

time: 45.1 us -> 43.7 us (0.969)
  Pallas kernels: 43.2 us -> 41.8 us
    pallas_call x1, Pallas kernels: 43.2 us -> 41.8 us  [fused(): pl.pallas_call(functools.partial(kernel, n_seq, n_head), out_shape=jax.Sh...]
where the time goes in v2:
time: 43.7 us; the launch traced here: 43.6 us
  Pallas kernels  41.8 us (96%)
  local copies, waits for them, and re-layouts  1.72 us (4%)
    pallas_call x1, Pallas kernels, fused(): pl.pallas_call(functools.partial(kernel, n_seq, n_head), out_shape=jax.Sh...  41.8 us
    unnamed x1, local copies, waits for them, and re-layouts  1.72 us

profile of v2, /device:TPU:0, one launch (start us, length us, event | category | flops | bytes accessed | tf_op | source)
XLA Modules:
  0.0 43.6 jit_solution(8064258079572857990)
XLA Ops:
  0.0 41.8 %shard_map.64 = bf16[32,5120]{1,0:T(8,128)(2,1)} custom-call(bf16[32,4096]{1,0:T(8,128)(2,1)} %q_ref.1, bf16[32,4096]{1,0:T(8,128)(2,1)} %k_ref.1, bf16[32,4096]{1,0:T(8,128)(2,1)} %v_ref.1, bf16[512,1024]{1,0:T(8,128)(2,1)} %tk_ref.1, bf16[512,1024]{1,0:T(8,128)(2,1)} %tv_ref.1, bf16[1024,5120]{1,0:T(8,128)(2,1)} %w_ref.1), custom_call_target="tpu_custom_call" | custom-call | tf_op jit(solution)/shard_map/pallas_call | solution.py:222
  41.8 1.7 %copy.8 = bf16[32,5120]{1,0:T(8,128)(2,1)} copy(bf16[32,5120]{1,0:T(8,128)(2,1)} %shard_map.64) | data formatting | bytes 655360
